TPU v7x, 32 devices: a whole 2x2x4 slice. The times are simulated.
32 devices in a mesh: groups: 2 (over y), sp: 4 (over z), tp: 2 (over x), dp: 2 (over core).
Axes of the slice: x: 2, y: 2, z: 4, core: 2. Of those that a mesh axis runs over, the one named last changes fastest.
Arguments:
- queries: bfloat16 [4096, 4096], P(('groups', 'tp', 'dp', 'sp')), parts along dimension 0, may hold values from -6 to 6
- keys: bfloat16 [4096, 512], P(('groups', 'tp', 'dp', 'sp')), parts along dimension 0, may hold values from -6 to 6
- values: bfloat16 [4096, 512], P(('groups', 'tp', 'dp', 'sp')), parts along dimension 0, may hold values from -6 to 6
- doc_lengths: int32 [32], P('groups'), parts along dimension 0, may hold values from 1 to 256, 2048 in all
Outputs:
- attended: bfloat16 [4096, 4096], P(('groups', 'tp', 'dp', 'sp')), parts along dimension 0
There are 2 independent parts, one for each index of `groups`. A program takes and returns all parts, laid end to end along the dimension named above; each array names one. Nothing has to cross between parts.
Inputs may be any that keep to these rules, and one draw needn't show every extreme that they name: `doc_lengths`: 16 documents whose lengths sum to 2048; the longest has exactly 256 tokens.
All inputs are finite; a program needn't handle non-finite values.
Results may differ from a plain program's by a relative error of at most 0.0038.
Values may be sent and summed in bfloat16 or wider, within the bound.
A program may use at most 64 MiB of HBM per device.

v0:
```python
import functools
import math

import jax
import jax.numpy as jnp
from jax import lax
from jax.experimental import pallas as pl
from jax.experimental.pallas import tpu as pltpu
from jax.sharding import PartitionSpec as P

HEAD_SIZE = 128
MESH = pl.DeviceIdType.MESH
DEAD = -1e30


def place(index, dp_count, sp_count):
    return {
        "tp": index // (dp_count * sp_count),
        "dp": (index // sp_count) % dp_count,
        "sp": index % sp_count,
    }


def kernel(
    sizes, q_hbm, k_hbm, v_hbm, lengths_hbm, out_buf,
    q_buf, held, bias, lengths, q_sem, kv_sem, send_sem, recv_sem, lengths_sem,
):
    tp_count, dp_count, sp_count, hops, heads, group = sizes
    rows = q_hbm.shape[0]
    width = group * HEAD_SIZE
    blocks = tp_count * dp_count * sp_count
    me = (lax.axis_index("tp") * dp_count + lax.axis_index("dp")) * sp_count + lax.axis_index("sp")
    right = place(lax.rem(me + 1, blocks), dp_count, sp_count)
    left = place(lax.rem(me + blocks - 1, blocks), dp_count, sp_count)

    def load(source, which, head):
        columns = pl.ds(head * HEAD_SIZE, HEAD_SIZE)
        return pltpu.make_async_copy(
            source.at[:, columns], held.at[0, head, which], kv_sem.at[head, which]
        )

    def load_q(head):
        columns = pl.ds(head * width, width)
        return pltpu.make_async_copy(q_hbm.at[:, columns], q_buf.at[:, columns], q_sem.at[head])

    def send(hop, head):
        return pltpu.make_async_remote_copy(
            src_ref=held.at[hop, head],
            dst_ref=held.at[hop + 1, head],
            send_sem=send_sem.at[hop, head],
            recv_sem=recv_sem.at[hop, head],
            device_id=right,
            device_id_type=MESH,
        )

    def start_send(hop, head):
        @pl.when((me >= hop) & (me < blocks - 1))
        def _():
            send(hop, head).start()

    def wait_receive(hop, head):
        @pl.when(me >= hop)
        def _():
            send(hop - 1, head).wait_recv()

    get_lengths = pltpu.make_async_copy(lengths_hbm, lengths, lengths_sem)
    for head in range(heads):
        load(k_hbm, 0, head).start()
        load(v_hbm, 1, head).start()
    for head in range(heads):
        load_q(head).start()
    get_lengths.start()

    barrier = pltpu.get_barrier_semaphore()

    @pl.when(me > 0)
    def _():
        pl.semaphore_signal(barrier, inc=1, device_id=left, device_id_type=MESH)

    @pl.when(me < blocks - 1)
    def _():
        pl.semaphore_wait(barrier, 1)

    for head in range(heads):
        load(k_hbm, 0, head).wait()
        load(v_hbm, 1, head).wait()
        start_send(0, head)
    for hop in range(1, hops + 1):

        @pl.when(me < hop)
        def _():
            held[hop] = jnp.zeros_like(held[hop])

    get_lengths.wait()
    base = me * rows
    row = lax.broadcasted_iota(jnp.int32, (rows, rows), 0)
    column = lax.broadcasted_iota(jnp.int32, (rows, rows), 1)
    near = column <= row
    first = jnp.zeros((rows, rows), jnp.int32)
    end = jnp.int32(0)
    for entry in range(lengths.shape[0]):
        end = end + lengths[entry]
        first = jnp.where(base + row >= end, end, first)
    mixed_position = base + column - jnp.where(near, 0, hops * rows)
    bias[0] = jnp.where(mixed_position >= first, 0.0, DEAD)
    for hop in range(1, hops):
        bias[hop] = jnp.where(base - hop * rows + column >= first, 0.0, DEAD)

    for hop in range(1, hops):
        for head in range(heads):
            wait_receive(hop, head)
            start_send(hop, head)

    factor = HEAD_SIZE ** (-0.5) * math.log2(math.e)
    span = (hops + 1) * rows
    batch = math.gcd(group, 8)
    for head in range(heads):
        wait_receive(hops, head)
        load_q(head).wait()
        k_all = held[:, head, 0].reshape(span, HEAD_SIZE)
        v_all = held[:, head, 1].reshape(span, HEAD_SIZE)
        for member in range(0, group, batch):
            at = [head * width + (member + other) * HEAD_SIZE for other in range(batch)]
            q_rows = jnp.concatenate([q_buf[:, a : a + HEAD_SIZE] for a in at], axis=0)
            score = lax.dot_general(
                q_rows, k_all, (((1,), (1,)), ((), ())), preferred_element_type=jnp.float32
            ).reshape(batch, rows, span)
            parts = [score[:, :, hop * rows : (hop + 1) * rows] for hop in range(hops + 1)]
            mixed = jnp.where(near, parts[0], parts[hops])
            parts = [part + bias[hop] for hop, part in enumerate([mixed] + parts[1:hops])]
            top = jnp.max(functools.reduce(jnp.maximum, parts), axis=2, keepdims=True)
            weights = [jnp.exp2((part - top) * factor) for part in parts]
            total = jnp.sum(sum(weights[1:], weights[0]), axis=2, keepdims=True)
            ends = [jnp.where(near, weights[0], 0.0), jnp.where(near, 0.0, weights[0])]
            weight = jnp.concatenate([ends[0]] + weights[1:] + [ends[1]], axis=2)
            weight = weight.astype(jnp.bfloat16).reshape(batch * rows, span)
            summed = jnp.dot(weight, v_all, preferred_element_type=jnp.float32)
            result = (summed.reshape(batch, rows, HEAD_SIZE) / total).astype(jnp.bfloat16)
            for other, a in enumerate(at):
                out_buf[:, a : a + HEAD_SIZE] = result[other]

    for hop in range(hops):
        for head in range(heads):

            @pl.when((me >= hop) & (me < blocks - 1))
            def _():
                send(hop, head).wait_send()


def solution(mesh):
    tp_count, dp_count, sp_count = (mesh.shape[axis] for axis in ("tp", "dp", "sp"))
    hops = max(sp_count // 2, 1)

    def local(queries, keys, values, doc_lengths):
        rows, width = queries.shape
        heads = keys.shape[1] // HEAD_SIZE
        group = width // keys.shape[1]
        sizes = (tp_count, dp_count, sp_count, hops, heads, group)
        hbm = pl.BlockSpec(memory_space=pltpu.HBM)
        return pl.pallas_call(
            functools.partial(kernel, sizes),
            out_shape=jax.ShapeDtypeStruct((rows, width), jnp.bfloat16),
            in_specs=[hbm, hbm, hbm, hbm],
            out_specs=pl.BlockSpec(memory_space=pltpu.VMEM),
            scratch_shapes=[
                pltpu.VMEM((rows, width), jnp.bfloat16),
                pltpu.VMEM((hops + 1, heads, 2, rows, HEAD_SIZE), jnp.bfloat16),
                pltpu.VMEM((hops, rows, rows), jnp.float32),
                pltpu.SMEM(doc_lengths.shape, jnp.int32),
                pltpu.SemaphoreType.DMA((heads,)),
                pltpu.SemaphoreType.DMA((heads, 2)),
                pltpu.SemaphoreType.DMA((hops, heads)),
                pltpu.SemaphoreType.DMA((hops, heads)),
                pltpu.SemaphoreType.DMA,
            ],
            compiler_params=pltpu.CompilerParams(collective_id=0, has_side_effects=True, vmem_limit_bytes=32 << 20),
        )(queries, keys, values, doc_lengths)

    spec = P(("groups", "tp", "dp", "sp"), None)
    return jax.shard_map(
        local, mesh=mesh, in_specs=(spec, spec, spec, P("groups")), out_specs=spec, check_vma=False
    )
```

profile of v0, /device:TPU:1, one launch (start us, length us, event | category | flops | bytes accessed | tf_op | source)
XLA Modules:
  0.0 22.4 jit_solution(15677070124408313313)
XLA Ops:
  0.0 0.0 copy-start
  0.0 1.2 %copy-done = bf16[128,4096]{1,0:T(8,128)(2,1)S(1)} copy-done((bf16[128,4096]{1,0:T(8,128)(2,1)S(1)}, bf16[128,4096]{1,0:T(8,128)(2,1)}, u32[]{:S(2)}) %copy-start) | copy-done | bytes 1048600
  1.2 0.0 copy-start.1
  1.2 0.9 %copy-done.1 = bf16[128,512]{1,0:T(8,128)(2,1)S(1)} copy-done((bf16[128,512]{1,0:T(8,128)(2,1)S(1)}, bf16[128,512]{1,0:T(8,128)(2,1)}, u32[]{:S(2)}) %copy-start.1) | copy-done | bytes 131096
  2.1 0.0 copy-start.2
  2.1 0.9 %copy-done.2 = bf16[128,512]{1,0:T(8,128)(2,1)S(1)} copy-done((bf16[128,512]{1,0:T(8,128)(2,1)S(1)}, bf16[128,512]{1,0:T(8,128)(2,1)}, u32[]{:S(2)}) %copy-start.2) | copy-done | bytes 131096
  3.0 0.0 copy-start.3
  3.0 0.7 %copy-done.3 = s32[16]{0:T(128)S(1)} copy-done((s32[16]{0:T(128)S(1)}, s32[16]{0:T(128)}, u32[]{:S(2)}) %copy-start.3) | copy-done | bytes 88
  3.7 17.7 %shard_map.46 = bf16[128,4096]{1,0:T(8,128)(2,1)S(1)} custom-call(bf16[128,4096]{1,0:T(8,128)(2,1)S(1)} %copy-done, bf16[128,512]{1,0:T(8,128)(2,1)S(1)} %copy-done.1, bf16[128,512]{1,0:T(8,128)(2,1)S(1)} %copy-done.2, s32[16]{0:T(128)S(1)} %copy-done.3), custom_call_target="tpu_custom_call" | custom-call | tf_op jit(solution)/shard_map/pallas_call | solution.py:160
  21.4 1.0 %copy.6 = bf16[128,4096]{1,0:T(8,128)(2,1)} copy(bf16[128,4096]{1,0:T(8,128)(2,1)S(1)} %shard_map.46) | data formatting | bytes 2097152
Async XLA Ops:
  0.0 1.2 %copy-start = (bf16[128,4096]{1,0:T(8,128)(2,1)S(1)}, bf16[128,4096]{1,0:T(8,128)(2,1)}, u32[]{:S(2)}) copy-start(bf16[128,4096]{1,0:T(8,128)(2,1)} %q_hbm.1) | copy-start | bytes 3145732
  1.2 0.9 %copy-start.1 = (bf16[128,512]{1,0:T(8,128)(2,1)S(1)}, bf16[128,512]{1,0:T(8,128)(2,1)}, u32[]{:S(2)}) copy-start(bf16[128,512]{1,0:T(8,128)(2,1)} %k_hbm.1) | copy-start | bytes 393220
  2.1 0.9 %copy-start.2 = (bf16[128,512]{1,0:T(8,128)(2,1)S(1)}, bf16[128,512]{1,0:T(8,128)(2,1)}, u32[]{:S(2)}) copy-start(bf16[128,512]{1,0:T(8,128)(2,1)} %v_hbm.1) | copy-start | bytes 393220
  3.0 0.7 %copy-start.3 = (s32[16]{0:T(128)S(1)}, s32[16]{0:T(128)}, u32[]{:S(2)}) copy-start(s32[16]{0:T(128)} %lengths_hbm.1) | copy-start | bytes 196
where the time goes:
time: 22.6 us; the launch traced here: 22.4 us
  Pallas kernels  17.7 us (78%)
  local copies, waits for them, and re-layouts  4.66 us (21%)
    pallas_call x1, Pallas kernels, local(): pl.pallas_call(functools.partial(kernel, sizes), out_shape=jax.ShapeDtype...  17.7 us
    unnamed x9, local copies, waits for them, and re-layouts  4.66 us

commit v1 on v0

--- a/solution.py
+++ b/solution.py
@@ -174,7 +174,7 @@
                 pltpu.SemaphoreType.DMA,
             ],
             compiler_params=pltpu.CompilerParams(collective_id=0, has_side_effects=True, vmem_limit_bytes=32 << 20),
-        )(queries, keys, values, doc_lengths)
+        )(*(pltpu.with_memory_space_constraint(x, pltpu.HBM) for x in (queries, keys, values, doc_lengths)))
 
     spec = P(("groups", "tp", "dp", "sp"), None)
     return jax.shard_map(

time: 22.6 us -> 19.8 us (0.88)
  local copies, waits for them, and re-layouts: 4.66 us -> 0.97 us
  Pallas kernels: 17.7 us -> 18.7 us
    unnamed x9 -> x1, local copies, waits for them, and re-layouts: 4.66 us -> 0.97 us
    pallas_call x1, Pallas kernels: 17.7 us -> 18.7 us  [local(): pl.pallas_call(functools.partial(kernel, sizes), out_shape=jax.ShapeDtype...]
where the time goes in v1:
time: 19.8 us; the launch traced here: 19.7 us
  Pallas kernels  18.7 us (94%)
  local copies, waits for them, and re-layouts  0.97 us (5%)
    pallas_call x1, Pallas kernels, local(): pl.pallas_call(functools.partial(kernel, sizes), out_shape=jax.ShapeDtype...  18.7 us
    unnamed x1, local copies, waits for them, and re-layouts  0.97 us

profile of v1, /device:TPU:1, one launch (start us, length us, event | category | flops | bytes accessed | tf_op | source)
XLA Modules:
  0.0 19.7 jit_solution(1722436660104332071)
XLA Ops:
  0.0 18.7 %shard_map.46 = bf16[128,4096]{1,0:T(8,128)(2,1)S(1)} custom-call(bf16[128,4096]{1,0:T(8,128)(2,1)} %q_hbm.1, bf16[128,512]{1,0:T(8,128)(2,1)} %k_hbm.1, bf16[128,512]{1,0:T(8,128)(2,1)} %v_hbm.1, s32[16]{0:T(128)} %lengths_hbm.1), custom_call_target="tpu_custom_call" | custom-call | tf_op jit(solution)/shard_map/pallas_call | solution.py:160
  18.7 1.0 %copy.6 = bf16[128,4096]{1,0:T(8,128)(2,1)} copy(bf16[128,4096]{1,0:T(8,128)(2,1)S(1)} %shard_map.46) | data formatting | bytes 2097152

commit v2 on v1

v2 whole, which is shorter than its diff:
```python
import functools
import math

import jax
import jax.numpy as jnp
from jax import lax
from jax.experimental import pallas as pl
from jax.experimental.pallas import tpu as pltpu
from jax.sharding import PartitionSpec as P

HEAD_SIZE = 128
MESH = pl.DeviceIdType.MESH
DEAD = -1e30


def kernel(
    sizes, q_hbm, k_hbm, v_hbm, lengths_hbm, out_buf,
    q_buf, held, stage, bias, top_buf, total_buf, summed_buf, lengths,
    q_sem, kv_sem, send_sem, far_sem, recv_sem, stage_sem, lengths_sem, ready_sem,
):
    tp_count, dp_count, sp_count, hops, heads, group = sizes
    rows = q_hbm.shape[0]
    lines = dp_count * sp_count
    blocks = tp_count * lines
    line, core, plane = (lax.axis_index(axis) for axis in ("sp", "dp", "tp"))
    me = (plane * dp_count + core) * sp_count + line

    def device(index):
        index = lax.rem(index + 2 * blocks, blocks)
        return {"tp": index // lines, "dp": (index // sp_count) % dp_count, "sp": index % sp_count}

    far = sp_count - line
    is_far = (far <= hops) & (me + far < blocks)
    crosses = core == dp_count - 1
    even = lax.rem(far, 2) == 0
    turns = is_far & crosses & even
    goes_far = is_far & jnp.logical_not(turns)
    relays = (far <= hops) & crosses & even & (plane >= 1)
    to_right = line < sp_count - 1
    right, left, turn, turned = device(me + 1), device(me - 1), device(me + lines), device(me - lines)
    far_target = device(me + far - jnp.where(relays, lines, 0))

    def far_sender(target, distance):
        return device(target - distance + (jnp.where(core == 0, lines, 0) if distance % 2 == 0 else 0))

    def load(head, which):
        source = (k_hbm, v_hbm)[which]
        return pltpu.make_async_copy(
            source.at[:, pl.ds(head * HEAD_SIZE, HEAD_SIZE)], held.at[0, head, which], kv_sem.at[head, which]
        )

    def load_q(head, member):
        return pltpu.make_async_copy(
            q_hbm.at[:, pl.ds((head * group + member) * HEAD_SIZE, HEAD_SIZE)],
            q_buf.at[head, pl.ds(member * rows, rows)],
            q_sem.at[head, member],
        )

    def copy(source, target, send, receive, where):
        return pltpu.make_async_remote_copy(
            src_ref=source, dst_ref=target, send_sem=send, recv_sem=receive, device_id=where, device_id_type=MESH
        )

    def forward(slot, head):
        return copy(
            held.at[slot, head], held.at[slot + 1, head], send_sem.at[slot, head], recv_sem.at[slot + 1, head], right
        )

    def send_far(head):
        return copy(held.at[0, head], held.at[far, head], far_sem.at[head], recv_sem.at[far, head], far_target)

    def send_turn(head):
        return copy(held.at[0, head], stage.at[head], far_sem.at[head], stage_sem.at[0, head], turn)

    def send_relay(head):
        return copy(stage.at[head], held.at[far, head], stage_sem.at[1, head], recv_sem.at[far, head], far_target)

    def receive(slot, head):
        pl.when(me >= slot)(forward(slot - 1, head).wait_recv)
        if slot < hops:
            pl.when(to_right & (me >= slot))(forward(slot, head).start)

    barrier = pltpu.get_barrier_semaphore()

    def greet(condition, where, semaphore=barrier):
        @pl.when(condition)
        def _():
            pl.semaphore_signal(semaphore, inc=1, device_id=where, device_id_type=MESH)

    def hear(condition):
        @pl.when(condition)
        def _():
            pl.semaphore_wait(ready_sem, 1)

    greet(line >= 1, left)
    greet((line == 0) & (me >= 1), far_sender(me, 1))
    greet(relays, turned)
    if hops > 1:
        greet((line == 0) & (me >= 2), right)
        greet((goes_far & to_right) | relays, device(me + far - jnp.where(relays, lines, 0) + 1))
    get_lengths = pltpu.make_async_copy(lengths_hbm, lengths, lengths_sem)
    for head in range(heads):
        for which in range(2):
            load(head, which).start()
    get_lengths.start()
    for head in range(heads):
        for member in range(group):
            load_q(head, member).start()
    meets = [to_right, goes_far & jnp.logical_not(to_right), turns]
    if hops > 1:
        introduced = [(line == 1) & (me > distance) for distance in range(2, hops + 1)]
        meets += [(line == 1) & (me >= 3)] + introduced
    peers = sum(condition.astype(jnp.int32) for condition in meets)

    @pl.when(peers > 0)
    def _():
        pl.semaphore_wait(barrier, peers)

    if hops > 1:
        for distance, condition in enumerate(introduced, 2):
            greet(condition, far_sender(me - 1, distance), ready_sem)
    for head in range(heads):
        for which in range(2):
            load(head, which).wait()
        pl.when(to_right)(forward(0, head).start)
        pl.when(goes_far & jnp.logical_not(to_right))(send_far(head).start)
        pl.when(turns)(send_turn(head).start)
    for slot in range(1, hops + 1):

        @pl.when(me < slot)
        def _():
            held[slot] = jnp.zeros_like(held[slot])

    get_lengths.wait()
    base = me * rows
    row = lax.broadcasted_iota(jnp.int32, (rows, rows), 0)
    column = lax.broadcasted_iota(jnp.int32, (rows, rows), 1)
    first = jnp.zeros((rows, rows), jnp.int32)
    end = jnp.int32(0)
    for entry in range(lengths.shape[0]):
        end = end + lengths[entry]
        first = jnp.where(base + row >= end, end, first)
    bias[0] = jnp.where((column <= row) & (base + column >= first), 0.0, DEAD)
    for slot in range(1, hops + 1):
        bias[slot] = jnp.where(base - slot * rows + column >= first, 0.0, DEAD)

    factor = HEAD_SIZE ** (-0.5) * math.log2(math.e)

    def weigh(step, slot, head):
        score = lax.dot_general(
            q_buf[head], held[slot, head, 0], (((1,), (1,)), ((), ())), preferred_element_type=jnp.float32
        )
        score = score.reshape(group, rows, rows) + bias[slot]
        top = jnp.max(score, axis=2, keepdims=True)
        fade = None
        if step > 0:
            before = top_buf[head].reshape(group, rows, HEAD_SIZE)
            top = jnp.maximum(top, before)
            fade = jnp.exp2((before - top) * factor)
        weight = jnp.exp2((score - top) * factor)
        total = jnp.sum(weight, axis=2, keepdims=True)
        if step > 0:
            total = total + total_buf[head].reshape(group, rows, HEAD_SIZE) * fade
        return weight.astype(jnp.bfloat16).reshape(group * rows, rows), top, total, fade

    def flat(x):
        return jnp.broadcast_to(x, (group, rows, HEAD_SIZE)).reshape(group * rows, HEAD_SIZE)

    for step in range(hops + 1):
        for head in range(heads):
            if step == 0:
                for member in range(group):
                    load_q(head, member).wait()
            else:
                if step == 1:
                    if head == 0:
                        hear(relays)

                    @pl.when(relays)
                    def _():
                        send_turn(head).wait_recv()
                        send_relay(head).start()

                receive(step, head)
            weight, top, total, fade = weigh(step, step, head)
            summed = jnp.dot(weight, held[step, head, 1], preferred_element_type=jnp.float32)
            if step < hops:
                top_buf[head] = flat(top)
                total_buf[head] = flat(total)
                summed_buf[head] = summed if step == 0 else summed_buf[head] * flat(fade) + summed
            else:
                inverse = 1.0 / flat(total)
                kept = summed_buf[head] * (flat(fade) * inverse)
                result = (kept + summed * inverse).astype(jnp.bfloat16)
                for member in range(group):
                    a = (head * group + member) * HEAD_SIZE
                    out_buf[:, a : a + HEAD_SIZE] = result[member * rows : (member + 1) * rows]

        if step == 0:
            hear(goes_far & to_right)

            @pl.when(goes_far & to_right)
            def _():
                for head in range(heads):
                    send_far(head).start()

    for head in range(heads):
        pl.when(to_right)(forward(0, head).wait_send)
        pl.when(goes_far)(send_far(head).wait_send)
        pl.when(turns)(send_turn(head).wait_send)
        pl.when(relays)(send_relay(head).wait_send)
        for slot in range(1, hops):
            pl.when(to_right & (me >= slot))(forward(slot, head).wait_send)


def solution(mesh):
    tp_count, dp_count, sp_count = (mesh.shape[axis] for axis in ("tp", "dp", "sp"))
    hops = max(sp_count // 2, 1)

    def local(queries, keys, values, doc_lengths):
        rows, width = queries.shape
        heads = keys.shape[1] // HEAD_SIZE
        group = width // keys.shape[1]
        sizes = (tp_count, dp_count, sp_count, hops, heads, group)
        hbm = pl.BlockSpec(memory_space=pltpu.HBM)
        arguments = (queries, keys, values, doc_lengths)
        return pl.pallas_call(
            functools.partial(kernel, sizes),
            out_shape=jax.ShapeDtypeStruct((rows, width), jnp.bfloat16),
            in_specs=[hbm, hbm, hbm, hbm],
            out_specs=pl.BlockSpec(memory_space=pltpu.VMEM),
            scratch_shapes=[
                pltpu.VMEM((heads, group * rows, HEAD_SIZE), jnp.bfloat16),
                pltpu.VMEM((hops + 1, heads, 2, rows, HEAD_SIZE), jnp.bfloat16),
                pltpu.VMEM((heads, 2, rows, HEAD_SIZE), jnp.bfloat16),
                pltpu.VMEM((hops + 1, rows, rows), jnp.float32),
                pltpu.VMEM((heads, group * rows, HEAD_SIZE), jnp.float32),
                pltpu.VMEM((heads, group * rows, HEAD_SIZE), jnp.float32),
                pltpu.VMEM((heads, group * rows, HEAD_SIZE), jnp.float32),
                pltpu.SMEM(doc_lengths.shape, jnp.int32),
                pltpu.SemaphoreType.DMA((heads, group)),
                pltpu.SemaphoreType.DMA((heads, 2)),
                pltpu.SemaphoreType.DMA((hops, heads)),
                pltpu.SemaphoreType.DMA((heads,)),
                pltpu.SemaphoreType.DMA((hops + 1, heads)),
                pltpu.SemaphoreType.DMA((2, heads)),
                pltpu.SemaphoreType.DMA,
                pltpu.SemaphoreType.REGULAR,
            ],
            compiler_params=pltpu.CompilerParams(collective_id=0, has_side_effects=True, vmem_limit_bytes=40 << 20),
        )(*(pltpu.with_memory_space_constraint(x, pltpu.HBM) for x in arguments))

    spec = P(("groups", "tp", "dp", "sp"), None)
    return jax.shard_map(
        local, mesh=mesh, in_specs=(spec, spec, spec, P("groups")), out_specs=spec, check_vma=False
    )
```

time: 19.8 us -> 17.3 us (0.87)
  Pallas kernels: 18.7 us -> 16.1 us
    pallas_call x1, Pallas kernels: 18.7 us -> 16.1 us  [local(): pl.pallas_call(functools.partial(kernel, sizes), out_shape=jax.ShapeDtype...]
where the time goes in v2:
time: 17.3 us; the launch traced here: 17.1 us
  Pallas kernels  16.1 us (93%)
  local copies, waits for them, and re-layouts  0.97 us (6%)
    pallas_call x1, Pallas kernels, local(): pl.pallas_call(functools.partial(kernel, sizes), out_shape=jax.ShapeDtype...  16.1 us
    unnamed x1, local copies, waits for them, and re-layouts  0.97 us

profile of v2, /device:TPU:1, one launch (start us, length us, event | category | flops | bytes accessed | tf_op | source)
XLA Modules:
  0.0 17.1 jit_solution(15651810905105418848)
XLA Ops:
  0.0 16.1 %shard_map.46 = bf16[128,4096]{1,0:T(8,128)(2,1)S(1)} custom-call(bf16[128,4096]{1,0:T(8,128)(2,1)} %q_hbm.1, bf16[128,512]{1,0:T(8,128)(2,1)} %k_hbm.1, bf16[128,512]{1,0:T(8,128)(2,1)} %v_hbm.1, s32[16]{0:T(128)} %lengths_hbm.1), custom_call_target="tpu_custom_call" | custom-call | tf_op jit(solution)/shard_map/pallas_call | solution.py:227
  16.2 1.0 %copy.6 = bf16[128,4096]{1,0:T(8,128)(2,1)} copy(bf16[128,4096]{1,0:T(8,128)(2,1)S(1)} %shard_map.46) | data formatting | bytes 2097152

commit v3 on v2

v3 whole, which is shorter than its diff:
```python
import functools
import math

import jax
import jax.numpy as jnp
from jax import lax
from jax.experimental import pallas as pl
from jax.experimental.pallas import tpu as pltpu
from jax.sharding import PartitionSpec as P

HEAD_SIZE = 128
MESH = pl.DeviceIdType.MESH
DEAD = -1e30


def kernel(
    sizes, q_hbm, k_hbm, v_hbm, lengths_hbm, out_buf,
    q_buf, held, stage, bias, top_buf, total_buf, summed_buf, lengths,
    q_sem, kv_sem, send_sem, far_sem, recv_sem, stage_sem, lengths_sem,
):
    tp_count, dp_count, sp_count, hops, heads, group = sizes
    rows = q_hbm.shape[0]
    lines = dp_count * sp_count
    blocks = tp_count * lines
    line, core, plane = (lax.axis_index(axis) for axis in ("sp", "dp", "tp"))
    me = (plane * dp_count + core) * sp_count + line

    def device(index):
        index = lax.rem(index + 2 * blocks, blocks)
        return {"tp": index // lines, "dp": (index // sp_count) % dp_count, "sp": index % sp_count}

    far = sp_count - line
    is_far = (far <= hops) & (me + far < blocks)
    crosses = core == dp_count - 1
    odd = lax.rem(far, 2) == 1
    turns = is_far & crosses & odd
    goes_far = is_far & jnp.logical_not(turns)
    relays = (far <= hops) & crosses & odd & (plane >= 1)
    to_right = line < sp_count - 1
    right, left, turn, turned = device(me + 1), device(me - 1), device(me + lines), device(me - lines)
    far_target = device(me + far - jnp.where(relays, lines, 0))

    def far_sender(target, distance):
        return device(target - distance + (jnp.where(core == 0, lines, 0) if distance % 2 == 1 else 0))

    def load(head, which):
        source = (k_hbm, v_hbm)[which]
        return pltpu.make_async_copy(
            source.at[:, pl.ds(head * HEAD_SIZE, HEAD_SIZE)], held.at[0, 2 * head + which], kv_sem.at[head]
        )

    get_q = pltpu.make_async_copy(q_hbm, q_buf, q_sem)

    def copy(source, target, send, receive, where):
        return pltpu.make_async_remote_copy(
            src_ref=source, dst_ref=target, send_sem=send, recv_sem=receive, device_id=where, device_id_type=MESH
        )

    pieces = [pl.ds(2 * head, 2) for head in range(heads)]

    def new_pieces(row, count=1):
        return [n for n, piece in enumerate(pieces) if row <= piece.start < row + count]

    def forward(slot, n):
        rows_of = pieces[n]
        return copy(
            held.at[slot, rows_of], held.at[slot + 1, rows_of], send_sem, recv_sem.at[slot, n], right
        )

    def send_far(n):
        rows_of = pieces[n]
        return copy(held.at[0, rows_of], held.at[far, rows_of], far_sem, recv_sem.at[far - 1, n], far_target)

    def send_turn(n):
        rows_of = pieces[n]
        return copy(held.at[0, rows_of], stage.at[rows_of], far_sem, stage_sem.at[n], turn)

    def send_relay(n):
        rows_of = pieces[n]
        return copy(stage.at[rows_of], held.at[far, rows_of], far_sem, recv_sem.at[far - 1, n], far_target)

    def receive(slot, n):
        pl.when(me >= slot)(forward(slot - 1, n).wait_recv)
        if slot < hops:
            pl.when(to_right & (me >= slot))(forward(slot, n).start)

    barrier = pltpu.get_barrier_semaphore()

    def greet(condition, where):
        @pl.when(condition)
        def _():
            pl.semaphore_signal(barrier, inc=1, device_id=where, device_id_type=MESH)

    greet(line >= 1, left)
    for distance in range(1, hops + 1):
        greet((line == 0) & (me >= distance), far_sender(me, distance))
    greet(relays, turned)
    get_lengths = pltpu.make_async_copy(lengths_hbm, lengths, lengths_sem)
    for head in range(heads):
        for which in range(2):
            load(head, which).start()
    peers = sum(condition.astype(jnp.int32) for condition in (to_right, goes_far, relays, turns))

    @pl.when(peers > 0)
    def _():
        pl.semaphore_wait(barrier, peers)

    for n, piece in enumerate(pieces):
        for head in range(piece.start // 2, (piece.start + piece.size) // 2):
            both = held.at[0, pl.ds(2 * head, 2)]
            pltpu.make_async_copy(both, both, kv_sem.at[head]).wait()
        pl.when(to_right)(forward(0, n).start)
        pl.when(turns)(send_turn(n).start)
        pl.when(goes_far & jnp.logical_not(to_right))(send_far(n).start)
    get_lengths.start()
    get_q.start()
    for slot in range(1, hops + 1):

        @pl.when(me < slot)
        def _():
            held[slot] = jnp.zeros_like(held[slot])

    get_lengths.wait()
    base = me * rows
    row = lax.broadcasted_iota(jnp.int32, (rows, rows), 0)
    column = lax.broadcasted_iota(jnp.int32, (rows, rows), 1)
    first = jnp.zeros((rows, rows), jnp.int32)
    end = jnp.int32(0)
    for entry in range(lengths.shape[0]):
        end = end + lengths[entry]
        first = jnp.where(base + row >= end, end, first)
    bias[0] = jnp.where((column <= row) & (base + column >= first), 0.0, DEAD)
    for slot in range(1, hops + 1):
        bias[slot] = jnp.where(base - slot * rows + column >= first, 0.0, DEAD)

    factor = HEAD_SIZE ** (-0.5) * math.log2(math.e)

    def weigh(step, slot, head):
        columns = [(head * group + member) * HEAD_SIZE for member in range(group)]
        queries = jnp.concatenate([q_buf[:, a : a + HEAD_SIZE] for a in columns], axis=0)
        score = lax.dot_general(
            queries, held[slot, 2 * head], (((1,), (1,)), ((), ())), preferred_element_type=jnp.float32
        )
        score = score.reshape(group, rows, rows) + bias[slot]
        top = jnp.max(score, axis=2, keepdims=True)
        fade = None
        if step > 0:
            before = top_buf[head].reshape(group, rows, HEAD_SIZE)
            top = jnp.maximum(top, before)
            fade = jnp.exp2((before - top) * factor)
        weight = jnp.exp2((score - top) * factor)
        total = jnp.sum(weight, axis=2, keepdims=True)
        if step > 0:
            total = total + total_buf[head].reshape(group, rows, HEAD_SIZE) * fade
        return weight.astype(jnp.bfloat16).reshape(group * rows, rows), top, total, fade

    def flat(x):
        return jnp.broadcast_to(x, (group, rows, HEAD_SIZE)).reshape(group * rows, HEAD_SIZE)

    def start_far(condition):
        @pl.when(goes_far & to_right & condition)
        def _():
            for n in range(len(pieces)):
                send_far(n).start()

    start_far(jnp.logical_not(crosses))
    get_q.wait()
    for step in range(hops + 1):
        for head in range(heads):
            if step > 0:
                if step == 1:

                    @pl.when(relays)
                    def _():
                        for n in new_pieces(2 * head, 2):
                            send_turn(n).wait_recv()
                            send_relay(n).start()

                for n in new_pieces(2 * head):
                    receive(step, n)
            weight, top, total, fade = weigh(step, step, head)
            if step > 0:
                for n in new_pieces(2 * head + 1):
                    receive(step, n)
            summed = jnp.dot(weight, held[step, 2 * head + 1], preferred_element_type=jnp.float32)
            if step < hops:
                top_buf[head] = flat(top)
                total_buf[head] = flat(total)
                summed_buf[head] = summed if step == 0 else summed_buf[head] * flat(fade) + summed
            else:
                inverse = 1.0 / flat(total)
                kept = summed_buf[head] * (flat(fade) * inverse)
                result = (kept + summed * inverse).astype(jnp.bfloat16)
                for member in range(group):
                    a = (head * group + member) * HEAD_SIZE
                    out_buf[:, a : a + HEAD_SIZE] = result[member * rows : (member + 1) * rows]
            if step == 1 and head == heads // 2:
                start_far(crosses)

    def wait_sent(condition, count, sem):
        for slots in range(1, hops + 1):

            @pl.when(condition & (count == slots))
            def _():
                sent = held.at[pl.ds(0, slots)]
                pltpu.make_async_copy(sent, sent, sem).wait()

    wait_sent(to_right, jnp.minimum(me + 1, hops), send_sem)
    wait_sent(goes_far | turns | relays, (goes_far | turns).astype(jnp.int32) + relays.astype(jnp.int32), far_sem)


def solution(mesh):
    tp_count, dp_count, sp_count = (mesh.shape[axis] for axis in ("tp", "dp", "sp"))
    hops = max(sp_count // 2, 1)

    def local(queries, keys, values, doc_lengths):
        rows, width = queries.shape
        heads = keys.shape[1] // HEAD_SIZE
        group = width // keys.shape[1]
        sizes = (tp_count, dp_count, sp_count, hops, heads, group)
        hbm = pl.BlockSpec(memory_space=pltpu.HBM)
        arguments = (queries, keys, values, doc_lengths)
        return pl.pallas_call(
            functools.partial(kernel, sizes),
            out_shape=jax.ShapeDtypeStruct((rows, width), jnp.bfloat16),
            in_specs=[hbm, hbm, hbm, hbm],
            out_specs=pl.BlockSpec(memory_space=pltpu.VMEM),
            scratch_shapes=[
                pltpu.VMEM((rows, width), jnp.bfloat16),
                pltpu.VMEM((hops + 1, 2 * heads, rows, HEAD_SIZE), jnp.bfloat16),
                pltpu.VMEM((2 * heads, rows, HEAD_SIZE), jnp.bfloat16),
                pltpu.VMEM((hops + 1, rows, rows), jnp.float32),
                pltpu.VMEM((heads, group * rows, HEAD_SIZE), jnp.float32),
                pltpu.VMEM((heads, group * rows, HEAD_SIZE), jnp.float32),
                pltpu.VMEM((heads, group * rows, HEAD_SIZE), jnp.float32),
                pltpu.SMEM(doc_lengths.shape, jnp.int32),
                pltpu.SemaphoreType.DMA,
                pltpu.SemaphoreType.DMA((heads,)),
                pltpu.SemaphoreType.DMA,
                pltpu.SemaphoreType.DMA,
                pltpu.SemaphoreType.DMA((hops, heads)),
                pltpu.SemaphoreType.DMA((heads,)),
                pltpu.SemaphoreType.DMA,
            ],
            compiler_params=pltpu.CompilerParams(collective_id=0, has_side_effects=True, vmem_limit_bytes=40 << 20),
        )(*(pltpu.with_memory_space_constraint(x, pltpu.HBM) for x in arguments))

    spec = P(("groups", "tp", "dp", "sp"), None)
    return jax.shard_map(
        local, mesh=mesh, in_specs=(spec, spec, spec, P("groups")), out_specs=spec, check_vma=False
    )
```

time: 17.3 us -> 16.4 us (0.948)
  the two profiles are of different devices: /device:TPU:1 before, /device:TPU:3 now
where the time goes in v3:
time: 16.4 us; the launch traced here: 16.3 us
  Pallas kernels  15.3 us (93%)
  local copies, waits for them, and re-layouts  0.97 us (6%)
    pallas_call x1, Pallas kernels, local(): pl.pallas_call(functools.partial(kernel, sizes), out_shape=jax.ShapeDtype...  15.3 us
    unnamed x1, local copies, waits for them, and re-layouts  0.97 us

profile of v3, /device:TPU:3, one launch (start us, length us, event | category | flops | bytes accessed | tf_op | source)
XLA Modules:
  0.0 16.3 jit_solution(7110300971045125070)
XLA Ops:
  0.0 15.3 %shard_map.46 = bf16[128,4096]{1,0:T(8,128)(2,1)S(1)} custom-call(bf16[128,4096]{1,0:T(8,128)(2,1)} %q_hbm.1, bf16[128,512]{1,0:T(8,128)(2,1)} %k_hbm.1, bf16[128,512]{1,0:T(8,128)(2,1)} %v_hbm.1, s32[16]{0:T(128)} %lengths_hbm.1), custom_call_target="tpu_custom_call" | custom-call | tf_op jit(solution)/shard_map/pallas_call | solution.py:223
  15.3 1.0 %copy.6 = bf16[128,4096]{1,0:T(8,128)(2,1)} copy(bf16[128,4096]{1,0:T(8,128)(2,1)S(1)} %shard_map.46) | data formatting | bytes 2097152

commit v4 on v3

--- a/solution.py
+++ b/solution.py
@@ -13,9 +13,49 @@
 DEAD = -1e30
 
 
+def queries_of(q_buf, head, group):
+    columns = [(head * group + member) * HEAD_SIZE for member in range(group)]
+    return jnp.concatenate([q_buf[:, a : a + HEAD_SIZE] for a in columns], axis=0)
+
+
+def attend(queries, keys, values, bias, before):
+    rows = keys.shape[0]
+    factor = HEAD_SIZE ** (-0.5) * math.log2(math.e)
+    score = lax.dot_general(queries, keys, (((1,), (1,)), ((), ())), preferred_element_type=jnp.float32)
+    score = (score.reshape(-1, rows, rows) + bias).reshape(-1, rows)
+    top = jnp.max(score, axis=1, keepdims=True)
+    if before is not None:
+        top_before, total_before, summed_before = before
+        top = jnp.maximum(top, top_before)
+        fade = jnp.exp2((top_before - top) * factor)
+    weight = jnp.exp2((score - top) * factor)
+    total = jnp.sum(weight, axis=1, keepdims=True)
+    summed = jnp.dot(weight.astype(jnp.bfloat16), values, preferred_element_type=jnp.float32)
+    if before is not None:
+        total = total + total_before * fade
+        summed = summed + summed_before * fade
+    return jnp.broadcast_to(top, summed.shape), jnp.broadcast_to(total, summed.shape), summed
+
+
+def finish(heads, group, done, q_buf, last_kv, last_bias, last_top, last_total, last_summed, out, result_buf, sem):
+    rows = last_kv.shape[1]
+    rest = (heads - 1) * group * HEAD_SIZE
+    for head in range(heads - 1):
+        columns = pl.ds(head * group * HEAD_SIZE, group * HEAD_SIZE)
+        pltpu.make_async_copy(done.at[:, columns], out.at[:, columns], sem).start()
+    before = last_top[...], last_total[...], last_summed[...]
+    _, total, summed = attend(queries_of(q_buf, heads - 1, group), last_kv[0], last_kv[1], last_bias[...], before)
+    result = (summed / total).astype(jnp.bfloat16)
+    for member in range(group):
+        result_buf[:, member * HEAD_SIZE : (member + 1) * HEAD_SIZE] = result[member * rows : (member + 1) * rows]
+    pltpu.make_async_copy(result_buf, out.at[:, pl.ds(rest, group * HEAD_SIZE)], sem).start()
+    pltpu.make_async_copy(done, out, sem).wait()
+
+
 def kernel(
-    sizes, q_hbm, k_hbm, v_hbm, lengths_hbm, out_buf,
-    q_buf, held, stage, bias, top_buf, total_buf, summed_buf, lengths,
+    sizes, q_hbm, k_hbm, v_hbm, lengths_hbm,
+    out_buf, q_buf, last_kv, last_bias, last_top, last_total, last_summed,
+    held, stage, bias, top_buf, total_buf, summed_buf, lengths,
     q_sem, kv_sem, send_sem, far_sem, recv_sem, stage_sem, lengths_sem,
 ):
     tp_count, dp_count, sp_count, hops, heads, group = sizes
@@ -58,9 +98,6 @@
 
     pieces = [pl.ds(2 * head, 2) for head in range(heads)]
 
-    def new_pieces(row, count=1):
-        return [n for n, piece in enumerate(pieces) if row <= piece.start < row + count]
-
     def forward(slot, n):
         rows_of = pieces[n]
         return copy(
@@ -105,13 +142,21 @@
     def _():
         pl.semaphore_wait(barrier, peers)
 
-    for n, piece in enumerate(pieces):
-        for head in range(piece.start // 2, (piece.start + piece.size) // 2):
-            both = held.at[0, pl.ds(2 * head, 2)]
-            pltpu.make_async_copy(both, both, kv_sem.at[head]).wait()
+    def start_far(condition, start, stop):
+        @pl.when(goes_far & to_right & condition)
+        def _():
+            for n in range(start, stop):
+                send_far(n).start()
+
+    for n in range(heads):
+        both = held.at[0, pl.ds(2 * n, 2)]
+        pltpu.make_async_copy(both, both, kv_sem.at[n]).wait()
+        if n == 0:
+            start_far(True, 0, 1)
         pl.when(to_right)(forward(0, n).start)
         pl.when(turns)(send_turn(n).start)
-        pl.when(goes_far & jnp.logical_not(to_right))(send_far(n).start)
+        pl.when(goes_far & jnp.logical_not(to_right) & (True if n < heads - 1 else plane == 0))(send_far(n).start)
+    start_far(jnp.logical_not(crosses), 1, heads)
     get_lengths.start()
     get_q.start()
     for slot in range(1, hops + 1):
@@ -133,69 +178,43 @@
     for slot in range(1, hops + 1):
         bias[slot] = jnp.where(base - slot * rows + column >= first, 0.0, DEAD)
 
-    factor = HEAD_SIZE ** (-0.5) * math.log2(math.e)
-
-    def weigh(step, slot, head):
-        columns = [(head * group + member) * HEAD_SIZE for member in range(group)]
-        queries = jnp.concatenate([q_buf[:, a : a + HEAD_SIZE] for a in columns], axis=0)
-        score = lax.dot_general(
-            queries, held[slot, 2 * head], (((1,), (1,)), ((), ())), preferred_element_type=jnp.float32
-        )
-        score = score.reshape(group, rows, rows) + bias[slot]
-        top = jnp.max(score, axis=2, keepdims=True)
-        fade = None
-        if step > 0:
-            before = top_buf[head].reshape(group, rows, HEAD_SIZE)
-            top = jnp.maximum(top, before)
-            fade = jnp.exp2((before - top) * factor)
-        weight = jnp.exp2((score - top) * factor)
-        total = jnp.sum(weight, axis=2, keepdims=True)
-        if step > 0:
-            total = total + total_buf[head].reshape(group, rows, HEAD_SIZE) * fade
-        return weight.astype(jnp.bfloat16).reshape(group * rows, rows), top, total, fade
-
-    def flat(x):
-        return jnp.broadcast_to(x, (group, rows, HEAD_SIZE)).reshape(group * rows, HEAD_SIZE)
-
-    def start_far(condition):
-        @pl.when(goes_far & to_right & condition)
-        def _():
-            for n in range(len(pieces)):
-                send_far(n).start()
-
-    start_far(jnp.logical_not(crosses))
+    last_bias[...] = bias[hops]
     get_q.wait()
     for step in range(hops + 1):
         for head in range(heads):
             if step > 0:
-                if step == 1:
+                if step == 1 and head == 0:
 
                     @pl.when(relays)
                     def _():
-                        for n in new_pieces(2 * head, 2):
+                        for n in range(heads):
                             send_turn(n).wait_recv()
                             send_relay(n).start()
 
-                for n in new_pieces(2 * head):
-                    receive(step, n)
-            weight, top, total, fade = weigh(step, step, head)
-            if step > 0:
-                for n in new_pieces(2 * head + 1):
-                    receive(step, n)
-            summed = jnp.dot(weight, held[step, 2 * head + 1], preferred_element_type=jnp.float32)
+                receive(step, head)
+            if step == hops and head == heads - 1:
+                last_kv[...] = held[hops, pl.ds(2 * head, 2)]
+                break
+            final = head == heads - 1
+            tops, totals, sums = (
+                (last_top, last_total, last_summed) if final
+                else (top_buf.at[head], total_buf.at[head], summed_buf.at[head])
+            )
+            before = None if step == 0 else (tops[...], totals[...], sums[...])
+            top, total, summed = attend(
+                queries_of(q_buf, head, group), held[step, 2 * head], held[step, 2 * head + 1], bias[step], before
+            )
             if step < hops:
-                top_buf[head] = flat(top)
-                total_buf[head] = flat(total)
-                summed_buf[head] = summed if step == 0 else summed_buf[head] * flat(fade) + summed
+                tops[...], totals[...], sums[...] = top, total, summed
             else:
-                inverse = 1.0 / flat(total)
-                kept = summed_buf[head] * (flat(fade) * inverse)
-                result = (kept + summed * inverse).astype(jnp.bfloat16)
+                result = (summed / total).astype(jnp.bfloat16)
                 for member in range(group):
                     a = (head * group + member) * HEAD_SIZE
                     out_buf[:, a : a + HEAD_SIZE] = result[member * rows : (member + 1) * rows]
-            if step == 1 and head == heads // 2:
-                start_far(crosses)
+            if step == 0 and head == heads - 1:
+                pl.when(goes_far & jnp.logical_not(to_right) & (plane > 0))(send_far(heads - 1).start)
+            if step == 1 and head == heads - 1:
+                start_far(crosses, 1, heads)
 
     def wait_sent(condition, count, sem):
         for slots in range(1, hops + 1):
@@ -220,19 +239,26 @@
         sizes = (tp_count, dp_count, sp_count, hops, heads, group)
         hbm = pl.BlockSpec(memory_space=pltpu.HBM)
         arguments = (queries, keys, values, doc_lengths)
-        return pl.pallas_call(
+        vmem = pl.BlockSpec(memory_space=pltpu.VMEM)
+        state = pltpu.VMEM((group * rows, HEAD_SIZE), jnp.float32)
+        passed = [
+            pltpu.VMEM((rows, width), jnp.bfloat16),
+            pltpu.VMEM((rows, width), jnp.bfloat16),
+            pltpu.VMEM((2, rows, HEAD_SIZE), jnp.bfloat16),
+            pltpu.VMEM((rows, rows), jnp.float32),
+            state, state, state,
+        ]
+        states = pltpu.VMEM((heads - 1, group * rows, HEAD_SIZE), jnp.float32)
+        parts = pl.pallas_call(
             functools.partial(kernel, sizes),
-            out_shape=jax.ShapeDtypeStruct((rows, width), jnp.bfloat16),
-            in_specs=[hbm, hbm, hbm, hbm],
-            out_specs=pl.BlockSpec(memory_space=pltpu.VMEM),
+            out_shape=[jax.ShapeDtypeStruct(x.shape, x.dtype) for x in passed],
+            in_specs=[hbm] * 4,
+            out_specs=[vmem] * len(passed),
             scratch_shapes=[
-                pltpu.VMEM((rows, width), jnp.bfloat16),
                 pltpu.VMEM((hops + 1, 2 * heads, rows, HEAD_SIZE), jnp.bfloat16),
                 pltpu.VMEM((2 * heads, rows, HEAD_SIZE), jnp.bfloat16),
                 pltpu.VMEM((hops + 1, rows, rows), jnp.float32),
-                pltpu.VMEM((heads, group * rows, HEAD_SIZE), jnp.float32),
-                pltpu.VMEM((heads, group * rows, HEAD_SIZE), jnp.float32),
-                pltpu.VMEM((heads, group * rows, HEAD_SIZE), jnp.float32),
+                states, states, states,
                 pltpu.SMEM(doc_lengths.shape, jnp.int32),
                 pltpu.SemaphoreType.DMA,
                 pltpu.SemaphoreType.DMA((heads,)),
@@ -242,8 +268,16 @@
                 pltpu.SemaphoreType.DMA((heads,)),
                 pltpu.SemaphoreType.DMA,
             ],
-            compiler_params=pltpu.CompilerParams(collective_id=0, has_side_effects=True, vmem_limit_bytes=40 << 20),
+            compiler_params=pltpu.CompilerParams(collective_id=0, has_side_effects=True, vmem_limit_bytes=32 << 20),
         )(*(pltpu.with_memory_space_constraint(x, pltpu.HBM) for x in arguments))
+        return pl.pallas_call(
+            functools.partial(finish, heads, group),
+            out_shape=jax.ShapeDtypeStruct((rows, width), jnp.bfloat16),
+            in_specs=[vmem] * len(passed),
+            out_specs=hbm,
+            scratch_shapes=[pltpu.VMEM((rows, group * HEAD_SIZE), jnp.bfloat16), pltpu.SemaphoreType.DMA],
+            compiler_params=pltpu.CompilerParams(vmem_limit_bytes=16 << 20),
+        )(*parts)
 
     spec = P(("groups", "tp", "dp", "sp"), None)
     return jax.shard_map(

time: 16.4 us -> 16.1 us (0.982)
  the two profiles are of different devices: /device:TPU:3 before, /device:TPU:10 now
where the time goes in v4:
time: 16.1 us; the launch traced here: 16 us
  Pallas kernels  16 us (99%)
    pallas_call x1, Pallas kernels, local(): pl.pallas_call(functools.partial(kernel, sizes), out_shape=[jax.ShapeDtyp...  14.6 us
    pallas_call x1, Pallas kernels, local(): pl.pallas_call(functools.partial(finish, heads, group), out_shape=jax.Sha...  1.37 us

profile of v4, /device:TPU:10, one launch (start us, length us, event | category | flops | bytes accessed | tf_op | source)
XLA Modules:
  0.0 16.0 jit_solution(8749460255693720564)
XLA Ops:
  0.0 14.6 %shard_map.46 = (bf16[128,4096]{1,0:T(8,128)(2,1)S(1)}, bf16[128,4096]{1,0:T(8,128)(2,1)S(1)}, bf16[2,128,128]{2,1,0:T(8,128)(2,1)S(1)}, f32[128,128]{1,0:T(8,12...) custom-call(bf16[128,4096]{1,0:T(8,128)(2,1)} %q_hbm.1, ...), custom_call_target="tpu_custom_call" | custom-call | tf_op jit(solution)/shard_map/pallas_call | solution.py:252
  14.6 1.4 %shard_map.47 = bf16[128,4096]{1,0:T(8,128)(2,1)} custom-call(bf16[128,4096]{1,0:T(8,128)(2,1)S(1)} %get-tuple-element.12.done, bf16[128,4096]{1,0:T(8,128)(2,1)S(1)} %get-tuple-element.13.q_buf, bf16[2,128,128]{2,1,0:T(8,128)(2,1)S(1)} %get-tuple-element.14.last_kv, f32[128,128]{1,0:T(8,128)S(1)} %get-tuple-element.15.last_bias, ...), custom_call_target="tpu_custom_call" | custom-call | tf_op jit(solution)/shard_map/pallas_call | solution.py:273

commit v5 on v4

--- a/solution.py
+++ b/solution.py
@@ -18,43 +18,43 @@
     return jnp.concatenate([q_buf[:, a : a + HEAD_SIZE] for a in columns], axis=0)
 
 
-def attend(queries, keys, values, bias, before):
+def weigh(queries, keys, bias, before):
     rows = keys.shape[0]
     factor = HEAD_SIZE ** (-0.5) * math.log2(math.e)
     score = lax.dot_general(queries, keys, (((1,), (1,)), ((), ())), preferred_element_type=jnp.float32)
     score = (score.reshape(-1, rows, rows) + bias).reshape(-1, rows)
-    top = jnp.max(score, axis=1, keepdims=True)
+    top, fade = jnp.max(score, axis=1, keepdims=True), None
     if before is not None:
-        top_before, total_before, summed_before = before
-        top = jnp.maximum(top, top_before)
-        fade = jnp.exp2((top_before - top) * factor)
+        top = jnp.maximum(top, before[0])
+        fade = jnp.exp2((before[0] - top) * factor)
     weight = jnp.exp2((score - top) * factor)
     total = jnp.sum(weight, axis=1, keepdims=True)
-    summed = jnp.dot(weight.astype(jnp.bfloat16), values, preferred_element_type=jnp.float32)
     if before is not None:
-        total = total + total_before * fade
-        summed = summed + summed_before * fade
-    return jnp.broadcast_to(top, summed.shape), jnp.broadcast_to(total, summed.shape), summed
-
-
-def finish(heads, group, done, q_buf, last_kv, last_bias, last_top, last_total, last_summed, out, result_buf, sem):
-    rows = last_kv.shape[1]
-    rest = (heads - 1) * group * HEAD_SIZE
-    for head in range(heads - 1):
-        columns = pl.ds(head * group * HEAD_SIZE, group * HEAD_SIZE)
+        total = total + before[1] * fade
+    return weight.astype(jnp.bfloat16), top, total, fade
+
+
+def finish(heads, group, done, last_values, last_weight, last_scale, last_kept, out, result_buf, sem):
+    rows = last_values.shape[1]
+    width = group * HEAD_SIZE
+    for head in range(heads - 2):
+        columns = pl.ds(head * width, width)
         pltpu.make_async_copy(done.at[:, columns], out.at[:, columns], sem).start()
-    before = last_top[...], last_total[...], last_summed[...]
-    _, total, summed = attend(queries_of(q_buf, heads - 1, group), last_kv[0], last_kv[1], last_bias[...], before)
-    result = (summed / total).astype(jnp.bfloat16)
-    for member in range(group):
-        result_buf[:, member * HEAD_SIZE : (member + 1) * HEAD_SIZE] = result[member * rows : (member + 1) * rows]
-    pltpu.make_async_copy(result_buf, out.at[:, pl.ds(rest, group * HEAD_SIZE)], sem).start()
+    for other in range(2):
+        summed = jnp.dot(last_weight[other], last_values[other], preferred_element_type=jnp.float32)
+        result = (summed * last_scale[other] + last_kept[other]).astype(jnp.bfloat16)
+        for member in range(group):
+            a = other * width + member * HEAD_SIZE
+            result_buf[:, a : a + HEAD_SIZE] = result[member * rows : (member + 1) * rows]
+        pltpu.make_async_copy(
+            result_buf.at[:, pl.ds(other * width, width)], out.at[:, pl.ds((heads - 2 + other) * width, width)], sem
+        ).start()
     pltpu.make_async_copy(done, out, sem).wait()
 
 
 def kernel(
     sizes, q_hbm, k_hbm, v_hbm, lengths_hbm,
-    out_buf, q_buf, last_kv, last_bias, last_top, last_total, last_summed,
+    out_buf, last_values, last_weight, last_scale, last_kept, q_buf,
     held, stage, bias, top_buf, total_buf, summed_buf, lengths,
     q_sem, kv_sem, send_sem, far_sem, recv_sem, stage_sem, lengths_sem,
 ):
@@ -83,10 +83,15 @@
     def far_sender(target, distance):
         return device(target - distance + (jnp.where(core == 0, lines, 0) if distance % 2 == 1 else 0))
 
+    split = heads - 2
+    row_of = [2 * head if head < split else split + head for head in range(heads)], [
+        2 * head + 1 if head < split else split + 2 + head for head in range(heads)
+    ]
+
     def load(head, which):
-        source = (k_hbm, v_hbm)[which]
+        source, at = (k_hbm, v_hbm)[which], row_of[which][head]
         return pltpu.make_async_copy(
-            source.at[:, pl.ds(head * HEAD_SIZE, HEAD_SIZE)], held.at[0, 2 * head + which], kv_sem.at[head]
+            source.at[:, pl.ds(head * HEAD_SIZE, HEAD_SIZE)], held.at[0, at], kv_sem.at[at // 2]
         )
 
     get_q = pltpu.make_async_copy(q_hbm, q_buf, q_sem)
@@ -96,7 +101,7 @@
             src_ref=source, dst_ref=target, send_sem=send, recv_sem=receive, device_id=where, device_id_type=MESH
         )
 
-    pieces = [pl.ds(2 * head, 2) for head in range(heads)]
+    pieces = [pl.ds(2 * n, 2) for n in range(heads)]
 
     def forward(slot, n):
         rows_of = pieces[n]
@@ -149,10 +154,10 @@
                 send_far(n).start()
 
     for n in range(heads):
-        both = held.at[0, pl.ds(2 * n, 2)]
+        both = held.at[0, pieces[n]]
         pltpu.make_async_copy(both, both, kv_sem.at[n]).wait()
-        if n == 0:
-            start_far(True, 0, 1)
+        if n < 2:
+            start_far(crosses | (n == 0), n, n + 1)
         pl.when(to_right)(forward(0, n).start)
         pl.when(turns)(send_turn(n).start)
         pl.when(goes_far & jnp.logical_not(to_right) & (True if n < heads - 1 else plane == 0))(send_far(n).start)
@@ -178,10 +183,13 @@
     for slot in range(1, hops + 1):
         bias[slot] = jnp.where(base - slot * rows + column >= first, 0.0, DEAD)
 
-    last_bias[...] = bias[hops]
+    def weigh_at(step, head):
+        before = None if step == 0 else (top_buf[head], total_buf[head])
+        return weigh(queries_of(q_buf, head, group), held[step, row_of[0][head]], bias[step], before)
+
     get_q.wait()
     for step in range(hops + 1):
-        for head in range(heads):
+        for head in range(split + 1):
             if step > 0:
                 if step == 1 and head == 0:
 
@@ -192,29 +200,33 @@
                             send_relay(n).start()
 
                 receive(step, head)
-            if step == hops and head == heads - 1:
-                last_kv[...] = held[hops, pl.ds(2 * head, 2)]
-                break
-            final = head == heads - 1
-            tops, totals, sums = (
-                (last_top, last_total, last_summed) if final
-                else (top_buf.at[head], total_buf.at[head], summed_buf.at[head])
-            )
-            before = None if step == 0 else (tops[...], totals[...], sums[...])
-            top, total, summed = attend(
-                queries_of(q_buf, head, group), held[step, 2 * head], held[step, 2 * head + 1], bias[step], before
-            )
-            if step < hops:
-                tops[...], totals[...], sums[...] = top, total, summed
-            else:
-                result = (summed / total).astype(jnp.bfloat16)
-                for member in range(group):
-                    a = (head * group + member) * HEAD_SIZE
-                    out_buf[:, a : a + HEAD_SIZE] = result[member * rows : (member + 1) * rows]
-            if step == 0 and head == heads - 1:
+            if step == 1 and head == 0:
                 pl.when(goes_far & jnp.logical_not(to_right) & (plane > 0))(send_far(heads - 1).start)
-            if step == 1 and head == heads - 1:
-                start_far(crosses, 1, heads)
+            weighed = [weigh_at(step, at) for at in ((head,) if head < split else (split, split + 1))]
+            if step == 1 and head == split:
+                start_far(crosses, 2, heads)
+            if head == split and step == hops:
+                for other, (weight, top, total, fade) in enumerate(weighed):
+                    scale = jnp.broadcast_to(1.0 / total, last_scale.shape[1:])
+                    last_weight[other], last_scale[other] = weight, scale
+                    last_kept[other] = summed_buf[split + other] * (fade * scale)
+            if head == split and step > 0:
+                receive(step, split + 1)
+            if head == split and step == hops:
+                last_values[...] = held[hops, pl.ds(row_of[1][split], 2)]
+                continue
+            for at, (weight, top, total, fade) in enumerate(weighed, head):
+                summed = jnp.dot(weight, held[step, row_of[1][at]], preferred_element_type=jnp.float32)
+                if step > 0:
+                    summed = summed + summed_buf[at] * fade
+                if step < hops:
+                    top_buf[at], total_buf[at] = (jnp.broadcast_to(x, summed.shape) for x in (top, total))
+                    summed_buf[at] = summed
+                else:
+                    result = (summed / total).astype(jnp.bfloat16)
+                    for member in range(group):
+                        a = (at * group + member) * HEAD_SIZE
+                        out_buf[:, a : a + HEAD_SIZE] = result[member * rows : (member + 1) * rows]
 
     def wait_sent(condition, count, sem):
         for slots in range(1, hops + 1):
@@ -240,21 +252,21 @@
         hbm = pl.BlockSpec(memory_space=pltpu.HBM)
         arguments = (queries, keys, values, doc_lengths)
         vmem = pl.BlockSpec(memory_space=pltpu.VMEM)
-        state = pltpu.VMEM((group * rows, HEAD_SIZE), jnp.float32)
+        state = pltpu.VMEM((2, group * rows, HEAD_SIZE), jnp.float32)
         passed = [
             pltpu.VMEM((rows, width), jnp.bfloat16),
-            pltpu.VMEM((rows, width), jnp.bfloat16),
             pltpu.VMEM((2, rows, HEAD_SIZE), jnp.bfloat16),
-            pltpu.VMEM((rows, rows), jnp.float32),
-            state, state, state,
+            pltpu.VMEM((2, group * rows, rows), jnp.bfloat16),
+            state, state,
         ]
-        states = pltpu.VMEM((heads - 1, group * rows, HEAD_SIZE), jnp.float32)
+        states = pltpu.VMEM((heads, group * rows, HEAD_SIZE), jnp.float32)
         parts = pl.pallas_call(
             functools.partial(kernel, sizes),
             out_shape=[jax.ShapeDtypeStruct(x.shape, x.dtype) for x in passed],
             in_specs=[hbm] * 4,
             out_specs=[vmem] * len(passed),
             scratch_shapes=[
+                pltpu.VMEM((rows, width), jnp.bfloat16),
                 pltpu.VMEM((hops + 1, 2 * heads, rows, HEAD_SIZE), jnp.bfloat16),
                 pltpu.VMEM((2 * heads, rows, HEAD_SIZE), jnp.bfloat16),
                 pltpu.VMEM((hops + 1, rows, rows), jnp.float32),
@@ -275,7 +287,7 @@
             out_shape=jax.ShapeDtypeStruct((rows, width), jnp.bfloat16),
             in_specs=[vmem] * len(passed),
             out_specs=hbm,
-            scratch_shapes=[pltpu.VMEM((rows, group * HEAD_SIZE), jnp.bfloat16), pltpu.SemaphoreType.DMA],
+            scratch_shapes=[pltpu.VMEM((rows, 2 * group * HEAD_SIZE), jnp.bfloat16), pltpu.SemaphoreType.DMA],
             compiler_params=pltpu.CompilerParams(vmem_limit_bytes=16 << 20),
         )(*parts)
 

time: 16.1 us -> 15.8 us (0.981)
  the two profiles are of different devices: /device:TPU:10 before, /device:TPU:14 now
where the time goes in v5:
time: 15.8 us; the launch traced here: 15.7 us
  Pallas kernels  15.7 us (99%)
    pallas_call x1, Pallas kernels, local(): pl.pallas_call(functools.partial(kernel, sizes), out_shape=[jax.ShapeDtyp...  14.6 us
    pallas_call x1, Pallas kernels, local(): pl.pallas_call(functools.partial(finish, heads, group), out_shape=jax.Sha...  1.08 us

profile of v5, /device:TPU:14, one launch (start us, length us, event | category | flops | bytes accessed | tf_op | source)
XLA Modules:
  0.0 15.7 jit_solution(11973146086908414589)
XLA Ops:
  0.0 14.6 %shard_map.46 = (bf16[128,4096]{1,0:T(8,128)(2,1)S(1)}, bf16[2,128,128]{2,1,0:T(8,128)(2,1)S(1)}, bf16[2,1024,128]{2,1,0:T(8,128)(2,1)S(1)}, f32[2,1024,128]{2,1,0:T(8,128)S(1)}, f32[2,1024,128]{2,1,0:T(8,128)S(1)}) custom-call(bf16[128,4096]{1,0:T(8,128)(2,1)} %q_hbm.1, bf16[128,512]{1,0:T(8,128)(2,1)} %k_hbm.1, bf16[128,512]{1,0:T(8,128)(2,1)} %v_hbm.1, ...), custom_call_target="tpu_custom_call" | custom-call | tf_op jit(solution)/shard_map/pallas_call | solution.py:263
  14.6 1.1 %shard_map.47 = bf16[128,4096]{1,0:T(8,128)(2,1)} custom-call(bf16[128,4096]{1,0:T(8,128)(2,1)S(1)} %get-tuple-element.10.done, bf16[2,128,128]{2,1,0:T(8,128)(2,1)S(1)} %get-tuple-element.11.last_values, bf16[2,1024,128]{2,1,0:T(8,128)(2,1)S(1)} %get-tuple-element.12.last_weight, f32[2,1024,128]{2,1,0:T(8,128)S(1)} %get-tuple-element.13.last_scale, ...), custom_call_target="tpu_custom_call" | custom-call | tf_op jit(solution)/shard_map/pallas_call | solution.py:285
